TPU v7x, 16 devices: a 4x2x1 block of a 4x4x8 slice. The times are simulated.
16 devices in a mesh: rep: 2 (over y, z), dp: 8 (over x, core).
Axes of the slice: x: 4, y: 2, z: 1, core: 2. Of those that a mesh axis runs over, the one named last changes fastest.
The devices are a block of a 4x4x8 slice.
Arguments:
- patches: bfloat16 [512, 256, 588], P(('rep', 'dp')), parts along dimension 0
- w_patch: bfloat16 [588, 384], P(None, 'dp')
- b_patch: bfloat16 [384], P('dp')
- pos_emb: bfloat16 [256, 384], P('dp')
- ln_scale: bfloat16 [384], P('dp')
- w_q: bfloat16 [384, 384], P('dp')
- w_k: bfloat16 [384, 384], P('dp')
- w_v: bfloat16 [384, 384], P('dp')
- q_scale: bfloat16 [64], replicated
- k_scale: bfloat16 [64], replicated
- w_out: bfloat16 [384, 384], P('dp')
- b_out: bfloat16 [384], P('dp')
- w_up: bfloat16 [384, 1536], P('dp')
- b_up: bfloat16 [1536], P('dp')
- w_down: bfloat16 [1536, 384], P('dp')
- b_down: bfloat16 [384], P('dp')
Outputs:
- output: bfloat16 [512, 256, 384], P(('rep', 'dp')), parts along dimension 0
There are 2 independent parts. A program takes and returns all parts, laid end to end along the dimension named above; an argument that names none is the same for every part.
All inputs are finite; a program needn't handle non-finite values.
Results may differ from a plain program's by a relative error of at most 0.00971256.
Values are sent between devices in bfloat16 or wider.
A program may use at most 768 MiB of HBM per device.

v0:
```python
import jax
import jax.numpy as jnp
from jax import lax
from jax.sharding import PartitionSpec as P

NORM_EPS = 1e-6


def layer_norm(x_f32, scale):
    mean = jnp.mean(x_f32, axis=-1, keepdims=True)
    centered = x_f32 - mean
    variance = jnp.mean(centered * centered, axis=-1, keepdims=True)
    return centered * lax.rsqrt(variance + NORM_EPS) * scale.astype(jnp.float32)


def gather_rows(shard):
    return lax.all_gather(shard, "dp", axis=0, tiled=True)


def solution(mesh):
    act_spec = P(("rep", "dp"), None, None)
    row_spec = P("dp", None)
    vec_spec = P("dp")
    in_specs = (act_spec, P(None, "dp"), vec_spec, row_spec, vec_spec, row_spec, row_spec, row_spec, P(None), P(None), row_spec, vec_spec, row_spec, vec_spec, row_spec, vec_spec)

    def per_device(patches, w_patch, b_patch, pos_emb, ln_scale, w_q, w_k, w_v, q_scale, k_scale, w_out, b_out, w_up, b_up, w_down, b_down):
        images = patches.shape[0]
        tokens = patches.shape[1]
        full_patch = lax.all_gather(w_patch, "dp", axis=1, tiled=True)
        width = full_patch.shape[1]
        head_dim = q_scale.shape[0]
        n_heads = width // head_dim
        embed = (jnp.einsum("btp,pd->btd", patches, full_patch, preferred_element_type=jnp.float32) + gather_rows(b_patch).astype(jnp.float32) + gather_rows(pos_emb).astype(jnp.float32)).astype(jnp.bfloat16)
        embed_f32 = embed.astype(jnp.float32)
        normed = layer_norm(embed_f32, gather_rows(ln_scale)).astype(jnp.bfloat16)

        def project(w_rows):
            projected = jnp.einsum("btd,de->bte", normed, gather_rows(w_rows), preferred_element_type=jnp.float32)
            return projected.astype(jnp.bfloat16).reshape(images, tokens, n_heads, head_dim)

        queries = layer_norm(project(w_q).astype(jnp.float32), q_scale).astype(jnp.bfloat16)
        key_heads = layer_norm(project(w_k).astype(jnp.float32), k_scale).astype(jnp.bfloat16)
        values = project(w_v)
        scores = jnp.einsum("bqhd,bkhd->bhqk", queries, key_heads, preferred_element_type=jnp.float32) * head_dim ** -0.5
        attn_probs = jax.nn.softmax(scores, axis=-1).astype(jnp.bfloat16)
        attended = jnp.einsum("bhqk,bkhd->bqhd", attn_probs, values, preferred_element_type=jnp.float32).astype(jnp.bfloat16).reshape(images, tokens, width)
        attn_out = jnp.einsum("btd,de->bte", attended, gather_rows(w_out), preferred_element_type=jnp.float32) + gather_rows(b_out).astype(jnp.float32)
        hidden = jnp.einsum("btd,df->btf", normed, gather_rows(w_up), preferred_element_type=jnp.float32) + gather_rows(b_up).astype(jnp.float32)
        hidden = jax.nn.gelu(hidden, approximate=False).astype(jnp.bfloat16)
        mlp_out = jnp.einsum("btf,fd->btd", hidden, gather_rows(w_down), preferred_element_type=jnp.float32) + gather_rows(b_down).astype(jnp.float32)
        return (embed_f32 + attn_out + mlp_out).astype(jnp.bfloat16)

    return jax.shard_map(per_device, mesh=mesh, in_specs=in_specs, out_specs=act_spec, check_vma=False)
```

profile of v0, /device:TPU:112, one launch (start us, length us, event | category | flops | bytes accessed | tf_op | source)
XLA Modules:
  0.0 497.5 jit_solution(902192400470855706)
XLA Ops:
  6.5 0.0 all-gather.3.cloned.1.call-start
  6.6 0.7 all-gather.3.cloned.1.call-update
  7.3 0.1 all-gather.5.cloned.1.call-start
  7.4 0.7 all-gather.5.cloned.1.call-update
  8.1 1.2 dynamic-slice
  10.7 0.9 dynamic-update-slice
  11.5 0.8 dynamic-update-slice.1
  12.4 0.8 dynamic-update-slice.2
  13.2 0.8 dynamic-update-slice.4
  14.1 0.8 dynamic-update-slice.3
  14.9 16.4 %all-reduce.5 = (bf16[384]{0:T(512)(128)(2,1)S(1)}, bf16[384]{0:T(512)(128)(2,1)S(1)}, bf16[384]{0:T(512)(128)(2,1)S(1)}, bf16[384]{0:T(512)(128)(2,1)S(1)}, bf16[1536]{0:T(1024)(128)(2,1)S(1)}) all-reduce(bf16[384]{0:T(512)(128)(2,1)S(1)} %dynamic-update-slice, ...), channel_id=1, replica_groups=mesh['rep'=2,'dp'=8] {'dp'}, use_global_device_ids=true, to_apply=%add | all-reduce | flops 3072 | bytes 12288
  31.3 21.5 %all_gather.41 = bf16[256,384]{1,0:T(8,128)(2,1)S(1)} all-gather(bf16[32,384]{1,0:T(8,128)(2,1)} %param.19), channel_id=1, replica_groups=mesh['rep'=2,'dp'=8] {'dp'}, dimensions={0}, use_global_device_ids=true | all-gather | bytes 221184 | tf_op jit(solution)/shard_map/all_gather | solution.py:17
  52.9 23.6 %all_gather.39 = bf16[588,384]{0,1:T(8,128)(2,1)S(1)} all-gather(bf16[588,48]{0,1:T(8,128)(2,1)} %param.17), channel_id=1, replica_groups=mesh['rep'=2,'dp'=8] {'dp'}, dimensions={1}, use_global_device_ids=true | all-gather | bytes 508032 | tf_op jit(solution)/shard_map/all_gather | solution.py:29
  76.5 0.0 copy-start.1
  76.5 13.9 %convert_reduce_fusion.2 = (f32[32,256]{1,0:T(8,128)S(1)}, bf16[32,256,384]{2,1,0:T(8,128)(2,1)S(1)}) fusion(f32[256,384]{1,0:T(8,128)S(1)} %convert_element_type.76, f32[384]{0:T(512)S(1)} %convert_element_type.75, bf16[588,384]{0,1:T(8,128)(2,1)S(1)} %all_gather.39, bf16[32,256,588]{1,0,2:T(8,128)(2,1)} %param.16), kind=kOutput, calls=%fused_computation.32 | convolution fusion | flops 3715096576 | bytes 16804352 | tf_op jit(solution)/shard_map/btp,pd->btd/dot_general | solution.py:33
  90.5 0.0 copy-start
  90.5 3.0 fusion.19
  93.6 0.0 copy-done.1
  93.6 22.1 %all_gather.44 = bf16[384,384]{1,0:T(8,128)(2,1)S(1)} all-gather(bf16[48,384]{1,0:T(8,128)(2,1)S(1)} %copy-done.1), channel_id=1, replica_groups=mesh['rep'=2,'dp'=8] {'dp'}, dimensions={0}, use_global_device_ids=true | all-gather | bytes 331776 | tf_op jit(solution)/shard_map/all_gather | solution.py:17
  115.6 0.0 copy-done
  115.6 7.4 %convert_convert_fusion.1 = f32[32,256,384]{2,1,0:T(8,128)} fusion(bf16[384,384]{1,0:T(8,128)(2,1)S(1)} %all_gather.44, bf16[32,256,384]{2,1,0:T(8,128)(2,1)S(1)} %get-tuple-element.13, f32[384]{0:T(512)S(1)} %convert_element_type.79, f32[32,256]{1,0:T(8,128)S(1)} %add_rsqrt_fusion.2, f32[32,256]{1,0:T(8,128)S(1)} %broadcast_multiply_fusion.2), kind=kOutput, calls=%fused_computation.49 | convolution fusion | flops 2437939200 | bytes 19236352 | tf_op jit(solution)/shard_map/btd,de->bte/dot_general | solution.py:38
  123.0 12.6 %copy.25 = f32[32,256,384]{1,2,0:T(8,128)} copy(f32[32,256,384]{2,1,0:T(8,128)} %convert_convert_fusion.1) | data formatting | bytes 25165824 | tf_op jit(solution)/shard_map/convert_element_type | solution.py:41
  135.6 0.0 copy-start.2
  135.6 0.0 slice-start
  135.6 6.7 %reduce_sum.65 = f32[32,256,6]{1,2,0:T(8,128)S(1)} reduce(f32[32,256,6,64]{1,3,2,0:T(8,128)} %bitcast.36, f32[]{:T(128)} %constant.35.clone.1), dimensions={3}, to_apply=%region_2.0 | reduce | flops 3096576 | bytes 12779524 | tf_op jit(solution)/shard_map/reduce_sum | solution.py:10
  142.3 0.0 slice-start.1
  142.3 7.9 %multiply_reduce_fusion.2 = f32[32,256,6]{1,2,0:T(8,128)S(1)} fusion(f32[32,256,6,64]{1,3,2,0:T(8,128)} %bitcast.37, f32[32,256,6]{1,2,0:T(8,128)S(1)} %broadcast_multiply_fusion.1), kind=kLoop, calls=%fused_computation.43 | loop fusion | flops 9388032 | bytes 12976128 | tf_op jit(solution)/shard_map/reduce_sum | solution.py:12
  150.2 0.0 copy-done.2
  150.2 23.3 %all_gather.45 = bf16[384,384]{1,0:T(8,128)(2,1)S(1)} all-gather(bf16[48,384]{1,0:T(8,128)(2,1)S(1)} %copy-done.2), channel_id=1, replica_groups=mesh['rep'=2,'dp'=8] {'dp'}, dimensions={0}, use_global_device_ids=true | all-gather | bytes 331776 | tf_op jit(solution)/shard_map/all_gather | solution.py:17
  173.5 0.0 slice-done
  173.5 0.0 slice-done.1
  173.5 7.4 %convert_convert_fusion = f32[32,256,384]{2,1,0:T(8,128)} fusion(bf16[384,384]{1,0:T(8,128)(2,1)S(1)} %all_gather.45, bf16[32,256,384]{2,1,0:T(8,128)(2,1)S(1)} %bitcast.44, f32[384]{0:T(512)S(1)} %convert_element_type.79, f32[32,256]{1,0:T(8,128)S(1)} %add_rsqrt_fusion.2, f32[32,256]{1,0:T(8,128)S(1)} %broadcast_multiply_fusion.2), kind=kOutput, calls=%fused_computation.48 | convolution fusion | flops 2437939200 | bytes 19236352 | tf_op jit(solution)/shard_map/btd,de->bte/dot_general | solution.py:38
  180.9 12.6 %copy.26 = f32[32,256,384]{1,2,0:T(8,128)} copy(f32[32,256,384]{2,1,0:T(8,128)} %convert_convert_fusion) | data formatting | bytes 25165824 | tf_op jit(solution)/shard_map/convert_element_type | solution.py:42
  193.4 0.0 copy-start.5
  193.4 0.0 copy-start.6
  193.4 0.0 copy-start.3
  193.4 0.0 slice-start.2
  193.5 6.7 %reduce_sum.67 = f32[32,256,6]{1,2,0:T(8,128)S(1)} reduce(f32[32,256,6,64]{1,3,2,0:T(8,128)} %bitcast.39, f32[]{:T(128)} %constant.35.clone.1), dimensions={3}, to_apply=%region_4.0 | reduce | flops 3096576 | bytes 12779524 | tf_op jit(solution)/shard_map/reduce_sum | solution.py:10
  200.2 0.0 slice-start.3
  200.2 7.9 %multiply_reduce_fusion.1 = f32[32,256,6]{1,2,0:T(8,128)S(1)} fusion(f32[32,256,6,64]{1,3,2,0:T(8,128)} %bitcast.40, f32[32,256,6]{1,2,0:T(8,128)S(1)} %broadcast_multiply_fusion), kind=kLoop, calls=%fused_computation.41 | loop fusion | flops 9388032 | bytes 12976128 | tf_op jit(solution)/shard_map/reduce_sum | solution.py:12
  208.1 0.0 copy-done.5
  208.1 0.0 copy-done.6
  208.1 0.0 copy-done.3
  208.1 21.6 %all_gather.43 = bf16[384,384]{1,0:T(8,128)(2,1)S(1)} all-gather(bf16[48,384]{1,0:T(8,128)(2,1)S(1)} %copy-done.3), channel_id=1, replica_groups=mesh['rep'=2,'dp'=8] {'dp'}, dimensions={0}, use_global_device_ids=true | all-gather | bytes 331776 | tf_op jit(solution)/shard_map/all_gather | solution.py:17
  229.7 0.0 slice-done.2
  229.7 0.0 slice-done.3
  229.8 0.0 copy-start.4
  229.8 6.5 %convolution_convert_fusion = bf16[32,256,384]{2,1,0:T(8,128)(2,1)} fusion(bf16[384,384]{1,0:T(8,128)(2,1)S(1)} %all_gather.43, bf16[32,256,384]{2,1,0:T(8,128)(2,1)S(1)} %bitcast.46, f32[384]{0:T(512)S(1)} %convert_element_type.79, f32[32,256]{1,0:T(8,128)S(1)} %add_rsqrt_fusion.2, f32[32,256]{1,0:T(8,128)S(1)} %broadcast_multiply_fusion.2), kind=kOutput, calls=%fused_computation.51 | convolution fusion | flops 2434793472 | bytes 12944896 | tf_op jit(solution)/shard_map/btd,de->bte/dot_general | solution.py:38
  236.2 8.6 %copy.24 = bf16[32,256,384]{1,2,0:T(8,128)(2,1)} copy(bf16[32,256,384]{2,1,0:T(8,128)(2,1)} %convolution_convert_fusion) | data formatting | bytes 12582912 | tf_op jit(solution)/shard_map/convert_element_type | solution.py:39
  244.9 0.0 copy-done.4
  244.9 23.3 %all_gather.46 = bf16[384,384]{1,0:T(8,128)(2,1)S(1)} all-gather(bf16[48,384]{1,0:T(8,128)(2,1)S(1)} %copy-done.4), channel_id=1, replica_groups=mesh['rep'=2,'dp'=8] {'dp'}, dimensions={0}, use_global_device_ids=true | all-gather | bytes 331776 | tf_op jit(solution)/shard_map/all_gather | solution.py:17
  268.1 0.1 add_rsqrt_fusion
  268.2 30.9 %fusion.78 = (f32[32,6,256]{2,1,0:T(8,128)S(1)}, f32[32,6,256,256]{2,3,1,0:T(8,128)}) fusion(f32[32,256,6,64]{1,3,2,0:T(8,128)} %bitcast.38, f32[64]{0:T(128)S(1)} %convert_element_type.85, f32[32,256,6]{1,2,0:T(8,128)S(1)} %get-tuple-element.18, f32[32,256,6]{1,2,0:T(8,128)S(1)} %broadcast_multiply_fusion.1, f32[32,256,6,64]{1,3,2,0:T(8,128)} %bitcast.41, ...), kind=kOutput, calls=%fused_computation.99 | convolution fusion | flops 1673527552 | bytes 76481024 | tf_op jit(solution)/shard_map/sub | solution.py:45
  299.2 21.8 %fusion.30 = bf16[32,6,64,256]{3,2,1,0:T(8,128)(2,1)} fusion(bf16[32,256,6,64]{1,3,2,0:T(8,128)(2,1)} %bitcast.47, f32[32,6,256,256]{2,3,1,0:T(8,128)} %get-tuple-element.15, f32[32,6,256]{2,1,0:T(8,128)S(1)} %get-tuple-element.14), kind=kOutput, calls=%fused_computation.50 | convolution fusion | flops 1638924288 | bytes 63111168 | tf_op jit(solution)/shard_map/bhqk,bkhd->bqhd/dot_general | solution.py:46
  321.0 11.3 %fusion.37 = f32[32,256,384]{2,1,0:T(8,128)} fusion(bf16[32,256,384]{1,2,0:T(8,128)(2,1)} %bitcast.42, bf16[384,384]{1,0:T(8,128)(2,1)S(1)} %all_gather.46), kind=kOutput, calls=%fused_computation.56 | convolution fusion | flops 2415919104 | bytes 19169280 | tf_op jit(solution)/shard_map/btd,de->bte/dot_general | solution.py:47
  332.3 0.0 all-gather.3.cloned.1.call-done
  332.3 37.5 %convert_reduce_fusion.1 = (u32[256,1536]{1,0:T(8,128)S(1)}, u32[256,1536]{1,0:T(8,128)S(1)}, f32[32,256,1536]{2,1,0:T(8,128)}) fusion(f32[1536]{0:T(1024)S(1)} %convert_element_type.96, bf16[384,1536]{1,0:T(8,128)(2,1)} %all-gather.3.cloned.1.call-done, bf16[32,256,384]{2,1,0:T(8,128)(2,1)} %copy-done, f32[384]{0:T(512)S(1)} %convert_element_type.79, ...), kind=kOutput, calls=%fused_computation.9 | convolution fusion | flops 9829613568 | bytes 61021696 | tf_op jit(solution)/shard_map/btd,df->btf/dot_general | solution.py:48
  369.8 0.0 all-gather.5.cloned.1.call-done
  369.8 120.5 %fusion.23 = bf16[32,256,384]{2,1,0:T(8,128)(2,1)} fusion(bf16[32,256,384]{2,1,0:T(8,128)(2,1)} %copy-done, f32[32,256,384]{2,1,0:T(8,128)} %fusion.37, f32[384]{0:T(512)S(1)} %convert_element_type.98, f32[384]{0:T(512)S(1)} %convert_element_type.95, f32[32,256,1536]{2,1,0:T(8,128)} %get-tuple-element.16, u32[256,1536]{1,0:T(8,128)S(1)} %get-tuple-element.6, ...), kind=kOutput, calls=%fused_computation.39 | convolution fusion | flops 10550771712 | bytes 79832064 | tf_op jit(solution)/shard_map/btf,fd->btd/dot_general | solution.py:50
  (19 shorter events, 0.1 us)
Async XLA Ops:
  6.5 325.7 %all-gather.3.cloned.1.call-start = ((), (), s32[]{:S(2)}) async-start(), calls=%async_computation | async-start | bytes 1327104 | tf_op jit(solution)/shard_map/all_gather | solution.py:17
  7.3 362.5 %all-gather.5.cloned.1.call-start = ((), (), s32[]{:S(2)}) async-start(), calls=%async_computation.1 | async-start | bytes 1327104 | tf_op jit(solution)/shard_map/all_gather | solution.py:17
  76.5 17.0 %copy-start.1 = (bf16[48,384]{1,0:T(8,128)(2,1)S(1)}, bf16[48,384]{1,0:T(8,128)(2,1)}, u32[]{:S(2)}) copy-start(bf16[48,384]{1,0:T(8,128)(2,1)} %param.21) | copy-start | bytes 110596
  90.5 25.2 %copy-start = (bf16[32,256,384]{2,1,0:T(8,128)(2,1)}, bf16[32,256,384]{2,1,0:T(8,128)(2,1)S(1)}, u32[]{:S(2)}) copy-start(bf16[32,256,384]{2,1,0:T(8,128)(2,1)S(1)} %get-tuple-element.13) | copy-start | bytes 18874372
  135.6 14.6 %copy-start.2 = (bf16[48,384]{1,0:T(8,128)(2,1)S(1)}, bf16[48,384]{1,0:T(8,128)(2,1)}, u32[]{:S(2)}) copy-start(bf16[48,384]{1,0:T(8,128)(2,1)} %param.22) | copy-start | bytes 110596
  135.6 37.9 %slice-start = ((s8[6291456]{0:T(1024)(128)(4,1)}), s8[2097152]{0:T(1024)(128)(4,1)S(1)}, s32[]{:S(2)}) async-start(s8[6291456]{0:T(1024)(128)(4,1)} %bitcast.43), calls=%async_computation.2 | async-start | bytes 4194304
  142.3 31.2 %slice-start.1 = ((s8[6291456]{0:T(1024)(128)(4,1)}), s8[4194304]{0:T(1024)(128)(4,1)S(1)}, s32[]{:S(2)}) async-start(s8[6291456]{0:T(1024)(128)(4,1)} %bitcast.43), calls=%async_computation.3 | async-start | bytes 8388608
  193.4 14.7 %copy-start.5 = (bf16[64]{0:T(256)(128)(2,1)S(1)}, bf16[64]{0:T(256)(128)(2,1)}, u32[]{:S(2)}) copy-start(bf16[64]{0:T(256)(128)(2,1)} %param.24) | copy-start | bytes 388
  193.4 14.7 %copy-start.6 = (bf16[64]{0:T(256)(128)(2,1)S(1)}, bf16[64]{0:T(256)(128)(2,1)}, u32[]{:S(2)}) copy-start(bf16[64]{0:T(256)(128)(2,1)} %param.25) | copy-start | bytes 388
  193.4 14.7 %copy-start.3 = (bf16[48,384]{1,0:T(8,128)(2,1)S(1)}, bf16[48,384]{1,0:T(8,128)(2,1)}, u32[]{:S(2)}) copy-start(bf16[48,384]{1,0:T(8,128)(2,1)} %param.23) | copy-start | bytes 110596
  193.4 36.3 %slice-start.2 = ((s8[6291456]{0:T(1024)(128)(4,1)}), s8[2097152]{0:T(1024)(128)(4,1)S(1)}, s32[]{:S(2)}) async-start(s8[6291456]{0:T(1024)(128)(4,1)} %bitcast.45), calls=%async_computation.4 | async-start | bytes 4194304
  200.2 29.6 %slice-start.3 = ((s8[6291456]{0:T(1024)(128)(4,1)}), s8[4194304]{0:T(1024)(128)(4,1)S(1)}, s32[]{:S(2)}) async-start(s8[6291456]{0:T(1024)(128)(4,1)} %bitcast.45), calls=%async_computation.5 | async-start | bytes 8388608
  229.8 15.1 %copy-start.4 = (bf16[48,384]{1,0:T(8,128)(2,1)S(1)}, bf16[48,384]{1,0:T(8,128)(2,1)}, u32[]{:S(2)}) copy-start(bf16[48,384]{1,0:T(8,128)(2,1)} %param.26) | copy-start | bytes 110596
Sparse Core Ops, SparseCore 0:
  8.9 22.2 all-gather.2
  32.8 19.5 all-gather.4
where the time goes:
time: 506 us; the launch traced here: 498 us
  matrix products  257 us (51%)
  blocking collectives  152 us (30%)
  local copies, waits for them, and re-layouts  39.3 us (8%)
  other arithmetic  32.4 us (6%)
  between operations  15.4 us (3%)
    dot_general x1, matrix products, per_device(): jnp.einsum('btf,fd->btd', hidden, gather_rows(w_down), preferred_element_...  120 us
    all_gather x5, blocking collectives, gather_rows(): return lax.all_gather(shard, 'dp', axis=0, tiled=True)  112 us
    dot_general x1, matrix products, per_device(): jnp.einsum('btd,df->btf', normed, gather_rows(w_up), preferred_element_ty...  37.5 us
    sub x1, matrix products, per_device(): attn_probs = jax.nn.softmax(scores, axis=-1).astype(jnp.bfloat16)  30.9 us
    all_gather x1, blocking collectives, per_device(): full_patch = lax.all_gather(w_patch, 'dp', axis=1, tiled=True)  23.6 us
    dot_general x1, matrix products, per_device(): jnp.einsum('bhqk,bkhd->bqhd', attn_probs, values, preferred_element_type=...  21.8 us
    dot_general x3, matrix products, project(): jnp.einsum('btd,de->bte', normed, gather_rows(w_rows), preferred_element_...  21.2 us
    reduce_sum x3, other arithmetic, layer_norm(): variance = jnp.mean(centered * centered, axis=-1, keepdims=True)  18.8 us
  transfers between devices with their start and end apart: 2, of which 0 were waited for; matrix products, arithmetic and copies ran while one was open for 42% of the time, Pallas kernels for 0%

commit v1 on v0

v1 whole, which is shorter than its diff:
```python
import functools
import math

import jax
import jax.numpy as jnp
from jax import lax
from jax.experimental import pallas as pl
from jax.experimental.pallas import tpu as pltpu
from jax.sharding import PartitionSpec as P

NORM_EPS = 1e-6
MESH = pl.DeviceIdType.MESH
BF16, F32 = jnp.bfloat16, jnp.float32
LANES = 128
GROUP = 8
ATTEND = 4
AHEAD = 2
MLP = 2
ONES_ROWS = 16
CORES = 2
VMEM_LIMIT = 60 * 1024 * 1024


def columns(row):
    return jnp.broadcast_to(row, (LANES, row.shape[1])).T


def norm_rows(x, gain):
    count = x.shape[0]
    mean = jnp.sum(x, axis=0, keepdims=True) * (1.0 / count)
    centered = x - mean
    variance = jnp.sum(centered * centered, axis=0, keepdims=True) * (1.0 / count)
    return centered * lax.rsqrt(variance + NORM_EPS) * gain


class Gather:
    def __init__(self, index, src, place, send, recv):
        self.index, self.src, self.place, self.send, self.recv = index, src, place, send, recv

    def copy(self, hop, src, block, target):
        return pltpu.make_async_remote_copy(
            src_ref=src, dst_ref=self.place(block), send_sem=self.send.at[self.index, hop],
            recv_sem=self.recv.at[self.index, hop], device_id={"dp": target}, device_id_type=MESH)


class Ring:
    def __init__(self, n):
        me = lax.axis_index("dp")
        self.chips = n // CORES
        self.chip, self.core = me // CORES, lax.rem(me, CORES)
        self.me = me
        self.sibling = self.device(self.chip, 1 - self.core)
        self.right = self.device(self.chip + 1, self.core)
        self.left = self.device(self.chip + self.chips - 1, self.core)
        self.onward = self.device(self.chip + 1 + self.core * (self.chips - 2), self.core)
        self.passed = self.device(self.chip + self.chips - 1 + self.core * (2 - self.chips), self.core)
        self.across = self.device(self.chip + 2, self.core)

    def device(self, chip, core):
        return lax.rem(chip, self.chips) * CORES + core

    def twin(self, device):
        return device + 1 - 2 * lax.rem(device, CORES)

    def start_own(self, items):
        for item in items:
            item.copy(1, item.src, self.me, self.right).start()
            item.copy(2, item.src, self.me, self.left).start()
            item.copy(0, item.src, self.me, self.sibling).start()

    def relay_near(self, items):
        for item in items:
            item.copy(1, item.src, self.left, self.right).wait_recv()
            item.copy(2, item.src, self.right, self.left).wait_recv()
            item.copy(5, item.place(self.passed), self.passed, self.onward).start()
            item.copy(3, item.place(self.left), self.left, self.sibling).start()
            item.copy(4, item.place(self.right), self.right, self.sibling).start()

    def relay_far(self, items):
        for item in items:
            item.copy(5, item.src, self.across, self.onward).wait_recv()
            item.copy(6, item.place(self.across), self.across, self.sibling).start()

    def finish(self, items):
        for item in items:
            for hop, block in ((0, self.me), (3, self.left), (4, self.right), (6, self.across)):
                item.copy(hop, item.src, self.twin(block), self.sibling).wait_recv()

    def drain(self, items):
        for item in items:
            for hop in range(7):
                item.copy(hop, item.src, self.me, self.sibling).wait_send()

    def barrier(self):
        semaphore = pltpu.get_barrier_semaphore()
        for other in (self.sibling, self.right, self.left):
            pl.semaphore_signal(semaphore, inc=1, device_id={"dp": other}, device_id_type=MESH)
        pl.semaphore_wait(semaphore, 3)


def first_kernel(n, heads, patches, wp, misc, wq, wk, wv, wo, wup, wdown, qs, ks,
                 e_out, h_out, o_out, w1_out, w2_out, vec_out,
                 g_wp, g_misc, g_q, g_k, g_v, g_o, g_u, g_d, w_qkv, bias_pos, gains, head_gains,
                 h_all, raw, q_pad, k_rows, v_ext, s_buf, p_buf, send, recv):
    step = pl.program_id(0)
    images, width, tokens = h_all.shape
    depth, group, _ = patches.shape
    slots = o_out.shape[0]
    embed_steps, attend_steps = images // group, images // slots
    head_dim = width // heads
    ring = Ring(n)

    def rows_of(ref, count):
        return lambda block: ref.at[pl.ds(pl.multiple_of(block * count, count), count), :]

    sources = (wp, misc, wq, wk, wv, wo, wup, wdown)
    targets = (g_wp, g_misc, g_q, g_k, g_v, g_o, g_u, g_d)
    items = [Gather(i, s, rows_of(t, s.shape[0]), send, recv) for i, (s, t) in enumerate(zip(sources, targets))]
    embed_items, qkv_items, late_items = items[:2], items[2:5], items[5:]

    def keep_own(some):
        for item in some:
            item.place(ring.me)[...] = item.src[...]

    @pl.when(step == 0)
    def _():
        ring.barrier()
        ring.start_own(embed_items)
        keep_own(items)
        ring.relay_near(embed_items)
        ring.start_own(qkv_items)
        ring.relay_far(embed_items)
        ring.finish(embed_items)
        pos_rows = tokens // n
        pos = jnp.concatenate([g_misc[b * misc.shape[0]:b * misc.shape[0] + pos_rows, :] for b in range(n)], axis=0).astype(F32)
        small = jnp.concatenate([g_misc[b * misc.shape[0] + pos_rows:(b + 1) * misc.shape[0], :].astype(F32)[0:1] for b in range(n)], axis=0)
        small = jnp.concatenate([small, jnp.zeros((LANES - n, width), F32)], axis=0).T
        piece = width // n

        def spread(first, count, b):
            return jnp.broadcast_to(small[first:first + count, b:b + 1], (count, LANES))

        for b in range(n):
            here = slice(b * piece, (b + 1) * piece)
            gains[0, here, :] = spread(0, piece, b)
            gains[1, here, :] = spread(piece, piece, b)
            vec_out[here, :] = spread(2 * piece, piece, b) + spread(3 * piece, piece, b)
            start = width + b * 4 * piece
            vec_out[start:start + 4 * piece, :] = spread(4 * piece, 4 * piece, b)
        pos_t = pos.T
        for i in range(tokens // LANES):
            bias_pos[:, i * LANES:(i + 1) * LANES] = gains[0] + pos_t[:, i * LANES:(i + 1) * LANES]
        head_gains[0] = columns(qs[...].astype(F32))[:head_dim]
        head_gains[1] = columns(ks[...].astype(F32))[:head_dim]
        v_ext[...] = jnp.ones_like(v_ext)
        q_pad[...] = jnp.zeros_like(q_pad)

    @pl.when(step == 1)
    def _():
        ring.relay_near(qkv_items)
        ring.start_own(late_items)

    @pl.when(step == embed_steps - 1)
    def _():
        ring.relay_far(qkv_items)

    @pl.when(step < embed_steps)
    def _():
        by_image = jnp.swapaxes(patches[...], 0, 1)
        for image in range(group):
            acc = jnp.dot(g_wp[:, :depth], by_image[image], preferred_element_type=F32)
            for lane in range(0, tokens, LANES):
                at = slice(lane, lane + LANES)
                e = (acc[:, at] + bias_pos[:, at]).astype(BF16)
                e_out[image, :, at] = e
                h = norm_rows(e.astype(F32), gains[1]).astype(BF16)
                h_all[step * group + image, :, at] = h
                h_out[image, :, at] = h

    scale = head_dim ** -0.5 * math.log2(math.e)
    units = slots * heads

    def project(kind, image, slot):
        out = jnp.dot(w_qkv[kind], h_all[image], preferred_element_type=F32).astype(BF16)
        if kind < 2:
            raw[slot, kind] = out
        else:
            for head in range(heads):
                v_ext[slot, head, :head_dim, :] = out[head * head_dim:(head + 1) * head_dim, :]

    def norm_heads(slot, couple):
        for lane in range(0, tokens, LANES):
            at = slice(lane, lane + LANES)
            keys = []
            for head in (2 * couple, 2 * couple + 1):
                rows = slice(head * head_dim, (head + 1) * head_dim)
                place = (head % 2) * head_dim
                q_pad[slot, head, place:place + head_dim, at] = norm_rows(raw[slot, 0, rows, at].astype(F32), head_gains[0]).astype(BF16)
                keys.append(norm_rows(raw[slot, 1, rows, at].astype(F32), head_gains[1]).astype(BF16))
            k_rows[slot, couple, at, :] = jnp.concatenate(keys, axis=0).T

    def score(unit):
        slot, head = divmod(unit % units, heads)
        s_buf[unit % s_buf.shape[0]] = jnp.dot(k_rows[slot, head // 2], q_pad[slot, head], preferred_element_type=F32)

    def soften(unit):
        for lane in range(0, tokens, LANES):
            at = slice(lane, lane + LANES)
            s = s_buf[unit % s_buf.shape[0], :, at]
            top = jnp.max(s, axis=0, keepdims=True)
            p_buf[unit % p_buf.shape[0], :, at] = jnp.exp2((s - top) * scale).astype(BF16)

    def attend(unit):
        slot, head = divmod(unit, heads)
        o = jnp.dot(v_ext[slot, head], p_buf[unit % p_buf.shape[0]], preferred_element_type=F32)
        o_out[slot, head * head_dim:(head + 1) * head_dim, :] = (o[:head_dim] * (1.0 / o[head_dim:head_dim + 1])).astype(BF16)

    @pl.when(step == embed_steps)
    def _():
        ring.finish(qkv_items)
        for i, ref in enumerate((g_q, g_k, g_v)):
            w_qkv[i] = ref[...].T
        ring.relay_near(late_items)
        for kind in range(3):
            project(kind, 0, 0)
        for couple in range(heads // 2):
            norm_heads(0, couple)
        for unit in range(AHEAD):
            score(unit)
        soften(0)

    @pl.when(step == embed_steps + attend_steps // 2)
    def _():
        ring.relay_far(late_items)

    @pl.when(step == embed_steps + attend_steps - 2)
    def _():
        ring.finish(late_items)
        ring.drain(items)
        w1_out[...] = g_u[...].T
        w2_out[:, :width] = g_o[...].T
        w2_out[:, width:] = g_d[...].T

    @pl.when(step >= embed_steps)
    def _():
        first = (step - embed_steps) * slots
        for slot in range(slots):
            following = jnp.minimum(first + slot + 1, images - 1)
            target = (slot + 1) % slots
            for head in range(heads):
                unit = slot * heads + head
                if head == 0:
                    project(0, following, target)
                    project(1, following, target)
                if head == 1:
                    project(2, following, target)
                score(unit + AHEAD)
                soften(unit + 1)
                if 1 <= head <= heads // 2:
                    norm_heads(target, head - 1)
                attend(unit)


def second_kernel(e, h, o, w1, w2, vec, y, z):
    images, tokens, width = y.shape
    hidden = w1.shape[0]
    root_half = math.sqrt(0.5)
    for image in range(images):
        z[image, :width, :] = o[image]
        for first in range(0, hidden, width):
            u = jnp.dot(w1[first:first + width, :], h[image], preferred_element_type=F32)
            for lane in range(0, tokens, LANES):
                x = u[:, lane:lane + LANES] + vec[width + first:2 * width + first, :]
                half = 0.5 * x
                z[image, width + first:2 * width + first, lane:lane + LANES] = (half + half * lax.erf(x * root_half)).astype(BF16)
    for image in range(images):
        acc = jnp.dot(w2[...], z[image], preferred_element_type=F32)
        for lane in range(0, tokens, LANES):
            at = slice(lane, lane + LANES)
            out = acc[:, at] + vec[:width, :] + e[image, :, at].astype(F32)
            y[image, at, :] = out.astype(BF16).T


def solution(mesh):
    n = mesh.shape["dp"]
    act_spec = P(("rep", "dp"), None, None)
    row_spec = P("dp", None)
    vec_spec = P("dp")
    in_specs = (act_spec, P(None, "dp"), vec_spec, row_spec, vec_spec, row_spec, row_spec, row_spec, P(None), P(None), row_spec, vec_spec, row_spec, vec_spec, row_spec, vec_spec)

    def per_device(patches, w_patch, b_patch, pos_emb, ln_scale, w_q, w_k, w_v, q_scale, k_scale, w_out, b_out, w_up, b_up, w_down, b_down):
        images, tokens, depth = patches.shape
        width = w_q.shape[1]
        hidden = w_up.shape[1]
        head_dim = q_scale.shape[0]
        heads = width // head_dim
        padded = -(-depth // LANES) * LANES
        wp = jnp.pad(w_patch.T, ((0, 0), (0, padded - depth)))
        small = jnp.concatenate([b_patch, ln_scale, b_out, b_down, b_up])
        small = jnp.pad(small[None, :], ((0, 15), (0, width - small.shape[0])))
        misc = jnp.concatenate([pos_emb, small], axis=0)

        whole = pl.BlockSpec(memory_space=pltpu.VMEM)
        embed_steps = images // GROUP
        attend_steps = images // ATTEND
        early = lambda s: (jnp.minimum(s, embed_steps - 1), 0, 0)
        late = lambda s: (jnp.maximum(s - embed_steps, 0), 0, 0)
        act = jax.ShapeDtypeStruct((images, width, tokens), BF16)
        shards = (wp, misc, w_q, w_k, w_v, w_out, w_up, w_down)
        e, h, o, w1, w2, vec = pl.pallas_call(
            functools.partial(first_kernel, n, heads),
            grid=(embed_steps + attend_steps,),
            out_shape=(act, act, act,
                       jax.ShapeDtypeStruct((hidden, width), BF16),
                       jax.ShapeDtypeStruct((width, width + hidden), BF16),
                       jax.ShapeDtypeStruct((width + hidden, LANES), F32)),
            in_specs=[pl.BlockSpec((depth, GROUP, tokens), lambda s: (0, jnp.minimum(s, embed_steps - 1), 0))] + [whole] * 10,
            out_specs=[pl.BlockSpec((GROUP, width, tokens), early)] * 2 + [
                       pl.BlockSpec((ATTEND, width, tokens), late), whole, whole, whole],
            scratch_shapes=[pltpu.VMEM((n * s.shape[0], s.shape[1]), BF16) for s in shards] + [
                pltpu.VMEM((3, width, width), BF16),
                pltpu.VMEM((width, tokens), F32),
                pltpu.VMEM((2, width, LANES), F32),
                pltpu.VMEM((2, head_dim, LANES), F32),
                pltpu.VMEM((images, width, tokens), BF16),
                pltpu.VMEM((ATTEND, 2, width, tokens), BF16),
                pltpu.VMEM((ATTEND, heads, 2 * head_dim, tokens), BF16),
                pltpu.VMEM((ATTEND, heads // 2, tokens, 2 * head_dim), BF16),
                pltpu.VMEM((ATTEND, heads, head_dim + ONES_ROWS, tokens), BF16),
                pltpu.VMEM((3, tokens, tokens), F32),
                pltpu.VMEM((2, tokens, tokens), BF16),
                pltpu.SemaphoreType.DMA((len(shards), 7)),
                pltpu.SemaphoreType.DMA((len(shards), 7)),
            ],
            compiler_params=pltpu.CompilerParams(collective_id=0, has_side_effects=True, vmem_limit_bytes=VMEM_LIMIT),
        )(jnp.transpose(patches, (2, 0, 1)), *shards, q_scale[None, :], k_scale[None, :])
        block = pl.BlockSpec((MLP, width, tokens), lambda s: (s, 0, 0))
        return pl.pallas_call(
            second_kernel,
            grid=(images // MLP,),
            out_shape=jax.ShapeDtypeStruct((images, tokens, width), BF16),
            in_specs=[block] * 3 + [whole] * 3,
            out_specs=pl.BlockSpec((MLP, tokens, width), lambda s: (s, 0, 0)),
            scratch_shapes=[pltpu.VMEM((MLP, width + hidden, tokens), BF16)],
            compiler_params=pltpu.CompilerParams(vmem_limit_bytes=VMEM_LIMIT),
        )(e, h, o, w1, w2, vec)

    return jax.shard_map(per_device, mesh=mesh, in_specs=in_specs, out_specs=act_spec, check_vma=False)
```

time: 506 us -> 107 us (0.21); the launches traced: 498 us -> 106 us
  matrix products: 257 us -> 0 us
  blocking collectives: 152 us -> 0 us
  Pallas kernels: 0 us -> 99.6 us
  local copies, waits for them, and re-layouts: 39.3 us -> 4.9 us
  other arithmetic: 32.4 us -> 1.36 us
  between operations: 15.4 us -> 0.01 us
    dot_general x8 -> x0, matrix products: 226 us -> none  [the longest x1 120 us: per_device(): jnp.einsum('btf,fd->btd', hidden, gather_rows(w_down), preferred_element_...]
    all_gather x6 -> x0, blocking collectives: 135 us -> none  [the longest x5 112 us: gather_rows(): return lax.all_gather(shard, 'dp', axis=0, tiled=True)]
    pallas_call x0 -> x2, Pallas kernels: none -> 99.6 us  [the longest x1 64.7 us: per_device(): pl.pallas_call(functools.partial(first_kernel, n, heads), grid=(embed_ste...]
    convert_element_type x3 -> x0, local copies, waits for them, and re-layouts: 33.7 us -> none  [the longest x1 12.6 us: per_device(): project(w_k).astype(jnp.float32)]
    reduce_sum x5 -> x0, other arithmetic: 32.2 us -> none  [the longest x3 18.8 us: layer_norm(): variance = jnp.mean(centered * centered, axis=-1, keepdims=True)]
    sub x1 -> x0, matrix products: 30.9 us -> none  [per_device(): attn_probs = jax.nn.softmax(scores, axis=-1).astype(jnp.bfloat16)]
    unnamed x1 -> x0, blocking collectives: 16.4 us -> none
    unnamed x33 -> x0, local copies, waits for them, and re-layouts: 5.54 us -> none
  transfers between devices with their start and end apart: 2 -> 0, of which waited for: 0 -> 0; matrix products, arithmetic and copies ran while one was open for 42% -> 0% of each run, Pallas kernels for 0% -> 0%
where the time goes in v1:
time: 107 us; the launch traced here: 106 us
  Pallas kernels  99.6 us (93%)
  local copies, waits for them, and re-layouts  4.9 us (5%)
  other arithmetic  1.36 us (1%)
    pallas_call x1, Pallas kernels, per_device(): pl.pallas_call(functools.partial(first_kernel, n, heads), grid=(embed_ste...  64.7 us
    pallas_call x1, Pallas kernels, per_device(): pl.pallas_call(second_kernel, grid=(images // MLP,), out_shape=jax.ShapeD...  34.9 us
    concatenate x1, local copies, waits for them, and re-layouts, per_device(): small = jnp.concatenate([b_patch, ln_scale, b_out, b_down, b_up])  3.43 us

profile of v1, /device:TPU:112, one launch (start us, length us, event | category | flops | bytes accessed | tf_op | source)
XLA Modules:
  0.0 105.8 jit_solution(996180683022964706)
XLA Ops:
  0.0 3.4 %concatenate.6 = bf16[384]{0:T(512)(128)(2,1)S(1)} concatenate(bf16[48]{0:T(256)(128)(2,1)} %param.18, bf16[48]{0:T(256)(128)(2,1)} %param.20, bf16[48]{0:T(256)(128)(2,1)} %param.27, bf16[48]{0:T(256)(128)(2,1)} %param.31, bf16[192]{0:T(256)(128)(2,1)} %param.29), dimensions={0} | concatenate | bytes 1536 | tf_op jit(solution)/shard_map/concatenate | solution.py:299
  3.4 1.4 %fusion.1.misc = bf16[48,384]{1,0:T(8,128)(2,1)} fusion(bf16[1,384]{1,0:T(2,128)(2,1)S(1)} %broadcast_in_dim.9, bf16[32,384]{1,0:T(8,128)(2,1)} %param.19), kind=kLoop, calls=%fused_computation.2 | loop fusion | flops 110592 | bytes 62208 | tf_op jit(solution)/shard_map/concatenate | solution.py:301
  4.8 1.5 %pad.8.wp = bf16[48,640]{1,0:T(8,128)(2,1)} pad(bf16[48,588]{1,0:T(8,128)(2,1)} %bitcast.5, bf16[]{:T(256)} %constant.2.clone.1), padding=0_0x0_52 | pad | bytes 117890 | tf_op jit(solution)/shard_map/jit(_pad)/pad | solution.py:298
  6.3 64.7 %shard_map.154 = (bf16[32,384,256]{2,1,0:T(8,128)(2,1)}, bf16[32,384,256]{2,1,0:T(8,128)(2,1)}, bf16[32,384,256]{2,1,0:T(8,128)(2,1)}, bf16[1536,384]{1,0:T(8,12...) custom-call(bf16[588,32,256]{2,1,0:T(8,128)(2,1)} %bitcast.4, bf16[48,640]{1,0:T(8,128)(2,1)} %pad.8.wp, ...), custom_call_target="tpu_custom_call" | custom-call | tf_op jit(solution)/shard_map/pallas_call | solution.py:310
  71.0 34.9 %shard_map.155 = bf16[32,256,384]{2,1,0:T(8,128)(2,1)} custom-call(bf16[32,384,256]{2,1,0:T(8,128)(2,1)} %get-tuple-element.11.e, bf16[32,384,256]{2,1,0:T(8,128)(2,1)} %get-tuple-element.12.h, bf16[32,384,256]{2,1,0:T(8,128)(2,1)} %get-tuple-element.13.o, bf16[1536,384]{1,0:T(8,128)(2,1)} %get-tuple-element.14.w1, bf16[384,1920]{1,0:T(8,128)(2,1)} %get-tuple-element.15.w2, ...), custom_call_target="tpu_custom_call" | custom-call | tf_op jit(solution)/shard_map/pallas_call | solution.py:338
  (1 shorter events, 0.0 us)
